TPU v7x, 128 devices: a whole 4x4x4 slice. The times are simulated.
128 devices in a mesh: row: 8 (over y, x_lo), col: 16 (over x_hi, z, core).
Axes of the slice: x: 4 (x_hi: 2, x_lo: 2; x = x_hi * 2 + x_lo), y: 4, z: 4, core: 2. Of those that a mesh axis runs over, the one named last changes fastest.
Arguments:
- features: bfloat16 [131072, 128], P(('row', 'col')), may hold values from -24 to 24
- tile_rows: int32 [8, 16, 1024], P('row', 'col'), may hold values from 0 to 127
- tile_cols: int32 [8, 16, 1024], P('row', 'col'), may hold values from 0 to 63
- edge_lists: int32 [2, 8, 16, 1024, 128], P(None, 'row', 'col'), may hold values from -16 to 127
- tile_counts: int32 [8, 16], P('row', 'col'), may hold values from 128 to 1024, as said below
Outputs:
- hop_one: bfloat16 [131072, 128], P(('row', 'col'))
- hop_two: bfloat16 [131072, 128], P(('row', 'col'))
Inputs may be any that keep to these rules, and one draw needn't show every extreme that they name: `tile_counts`: live tile slots of a block; some block has exactly 1024. `edge_lists`: a negative entry marks an empty edge slot; slots at or past a block's count hold arbitrary entries. `tile_rows`: a tile may occur in several slots; slots at or past a block's count hold arbitrary entries. `tile_cols`: slots at or past a block's count hold arbitrary entries.
All inputs are finite; a program needn't handle non-finite values.
Results may differ from a plain program's by a relative error of at most 0.0058.
Values may be sent and summed in bfloat16 or wider, within the bound.
A program may use at most 192 MiB of HBM per device.

v0:
```python
import functools

import jax
import jax.numpy as jnp
from jax import lax
from jax.experimental import pallas as pl
from jax.experimental.pallas import tpu as pltpu
from jax.sharding import PartitionSpec as P

TILE = 128
GROUP = 64
BATCH = 8
SUM_CHUNK = 8
RAW_CHUNK = 2
START_LIMIT = 42 * 2**20
APPLY_LIMIT = 34 * 2**20
SUM_LIMIT = 12 * 2**20
SUM_LAGS = (0, 2, 4, 6, 6, 8, 10, 10, 12)


MESH = pl.DeviceIdType.MESH


class Place:
    def __init__(self):
        self.row, self.col = lax.axis_index("row"), lax.axis_index("col")
        self.y, self.x_lo = self.row // 2, self.row % 2
        self.x_hi, self.z, self.core = self.col // 8, (self.col // 2) % 4, self.col % 2

    def at(self, y=None, x_lo=None, x_hi=None, z=None, core=None):
        pick = lambda new, old: old if new is None else new
        row = pick(y, self.y) * 2 + pick(x_lo, self.x_lo)
        col = (pick(x_hi, self.x_hi) * 4 + pick(z, self.z)) * 2 + pick(core, self.core)
        return (row, col)


def greet(devices):
    barrier = pltpu.get_barrier_semaphore()
    for device in devices:
        pl.semaphore_signal(barrier, inc=1, device_id=device, device_id_type=MESH)
    pl.semaphore_wait(barrier, len(devices))


def sum_devices(me):
    return [
        me.at(core=1 - me.core),
        me.at(z=(me.z + 1) % 4),
        me.at(z=(me.z + 3) % 4),
        me.at(x_hi=1 - me.x_hi),
    ]


def spread_devices(me):
    return [me.at(x_lo=1 - me.x_lo), me.at(y=(me.y + 1) % 4), me.at(y=(me.y + 3) % 4)]


def run_stages(stages, lags, chunks):
    for tick in range(max(lags) + chunks):
        for stage, lag in zip(stages, lags):
            if 0 <= tick - lag < chunks:
                stage(tick - lag)


def each_tile(q, chunks, body):
    size = 8 // chunks

    def step(i, carry):
        body(q * size + i)
        return carry

    lax.fori_loop(0, size, step, 0)


def span(q, chunks):
    return pl.ds(q * (8 // chunks), 8 // chunks)


def wide(x):
    return x.astype(jnp.float32)


def sum_stages(me, part, bufs, sems, finish):
    given, running, arrived, kept, across, crossed = bufs
    pair_send, pair_recv, ring_send, ring_recv, far_send, far_recv = sems
    chunks = SUM_CHUNK

    def pair_copy(q):
        return pltpu.make_async_remote_copy(
            part.at[:, :, 1 - me.core, span(q, chunks)], given.at[:, :, span(q, chunks)],
            pair_send.at[q], pair_recv.at[q],
            device_id=me.at(core=1 - me.core), device_id_type=MESH,
        )

    def ring_copy(half, step, q):
        up = (half == 0) == (step < 2)
        return pltpu.make_async_remote_copy(
            running.at[half, step, span(q, chunks)], arrived.at[half, step, span(q, chunks)],
            ring_send.at[half, step, q], ring_recv.at[half, step, q],
            device_id=me.at(z=(me.z + (1 if up else 3)) % 4), device_id_type=MESH,
        )

    def far_copy(q):
        return pltpu.make_async_remote_copy(
            across.at[span(q, chunks)], crossed.at[span(q, chunks)], far_send.at[q], far_recv.at[q],
            device_id=me.at(x_hi=1 - me.x_hi), device_id_type=MESH,
        )

    def begin():
        for q in range(chunks):
            pair_copy(q).start()

    def local_sum(half, offset, k):
        x_hi = me.x_hi if half == 0 else 1 - me.x_hi
        z = (me.z + (offset if half == 0 else 4 - offset)) % 4
        return part[x_hi, z, me.core, k] + given[x_hi, z, k]

    def first(q):
        pair_copy(q).wait_recv()
        for step, offset in ((0, 2), (2, 3)):
            for half in (1, 0):
                def body(k, half=half, step=step, offset=offset):
                    running[half, step, k] = local_sum(half, offset, k).astype(jnp.bfloat16)

                each_tile(q, chunks, body)
                ring_copy(half, step, q).start()

    def middle(q):
        for half in (1, 0):
            ring_copy(half, 0, q).wait_recv()

            def body(k, half=half):
                running[half, 1, k] = (local_sum(half, 1, k) + wide(arrived[half, 0, k])).astype(jnp.bfloat16)

            each_tile(q, chunks, body)
            ring_copy(half, 1, q).start()

    def last(q):
        for half in (1, 0):
            ring_copy(half, 2, q).wait_recv()
            ring_copy(half, 1, q).wait_recv()

            def body(k, half=half):
                total = local_sum(half, 0, k) + (wide(arrived[half, 1, k]) + wide(arrived[half, 2, k]))
                if half == 1:
                    across[k] = total.astype(jnp.bfloat16)
                else:
                    kept[k] = total

            each_tile(q, chunks, body)
            if half == 1:
                far_copy(q).start()

    def done(q):
        far_copy(q).wait_recv()
        each_tile(q, chunks, lambda k: finish(k, kept[k] + wide(crossed[k])))

    def drain():
        for q in range(chunks):
            pair_copy(q).wait_send()
            far_copy(q).wait_send()
            for half in (0, 1):
                for step in range(3):
                    ring_copy(half, step, q).wait_send()

    return begin, [first, middle, last, done], drain


def sum_scratch():
    block = lambda *lead, dtype=jnp.bfloat16: pltpu.VMEM((*lead, 8, TILE, TILE), dtype)
    dma = pltpu.SemaphoreType.DMA
    bufs = [block(2, 4, dtype=jnp.float32), block(2, 3), block(2, 3), block(dtype=jnp.float32), block(), block()]
    sems = [dma((SUM_CHUNK,))] * 2 + [dma((2, 3, SUM_CHUNK))] * 2 + [dma((SUM_CHUNK,))] * 2
    return bufs + sems


N_SUM = 12


def spread_stages(me, gathered, sems, chunks):
    side_send, side_recv, near_send, near_recv, relay_send, relay_recv, pass_send, pass_recv = sems

    def copy(block, send, recv, device):
        return pltpu.make_async_remote_copy(block, block, send, recv, device_id=device, device_id_type=MESH)

    def block(y, x_lo, q):
        return gathered.at[me.core, (me.y + y) % 4, me.x_lo if x_lo == 0 else 1 - me.x_lo, span(q, chunks)]

    def side_copy(q):
        return copy(block(0, 0, q), side_send.at[q], side_recv.at[q], me.at(x_lo=1 - me.x_lo))

    def near_copy(kind, way, q):
        device = me.at(y=(me.y + (1 if way == 0 else 3)) % 4)
        return copy(block(0, kind, q), near_send.at[kind, way, q], near_recv.at[kind, way, q], device)

    def relay_copy(way, q):
        device = me.at(y=(me.y + (1 if way == 0 else 3)) % 4)
        return copy(block(3 if way == 0 else 1, way, q), relay_send.at[way, q], relay_recv.at[way, q], device)

    def pass_copy(y, x_lo, q):
        return copy(block(y, x_lo, q), pass_send.at[y, x_lo, q], pass_recv.at[y, x_lo, q], me.at(core=1 - me.core))

    def own(q):
        side_copy(q).start()
        near_copy(0, 0, q).start()
        near_copy(0, 1, q).start()
        pass_copy(0, 0, q).start()

    def beside(q):
        side_copy(q).wait_recv()
        near_copy(1, 0, q).start()
        near_copy(1, 1, q).start()
        pass_copy(0, 1, q).start()

    def relay_own(q):
        near_copy(0, 0, q).wait_recv()
        relay_copy(0, q).start()
        pass_copy(3, 0, q).start()

    def relay_beside(q):
        near_copy(1, 1, q).wait_recv()
        relay_copy(1, q).start()
        pass_copy(1, 1, q).start()

    def opposite(q):
        near_copy(0, 1, q).wait_recv()
        pass_copy(1, 0, q).start()
        near_copy(1, 0, q).wait_recv()
        pass_copy(3, 1, q).start()
        for way in (0, 1):
            relay_copy(way, q).wait_recv()
            pass_copy(2, way, q).start()

    def drain():
        for q in range(chunks):
            for y in range(4):
                for x_lo in range(2):
                    pass_copy(y, x_lo, q).wait_recv()
        for q in range(chunks):
            side_copy(q).wait_send()
            for way in (0, 1):
                near_copy(0, way, q).wait_send()
                near_copy(1, way, q).wait_send()
                relay_copy(way, q).wait_send()
            for y in range(4):
                for x_lo in range(2):
                    pass_copy(y, x_lo, q).wait_send()

    return [own, beside, relay_own, relay_beside, opposite], drain


def spread_scratch(chunks):
    dma = pltpu.SemaphoreType.DMA
    return [dma((chunks,))] * 2 + [dma((2, 2, chunks))] * 2 + [dma((2, chunks))] * 2 + [dma((4, 2, chunks))] * 2


def hot(ids, cell):
    return jnp.where(jnp.broadcast_to(ids, (TILE, TILE)) == cell, jnp.bfloat16(1), jnp.bfloat16(0))


def narrow(x):
    return x.astype(jnp.float32).astype(jnp.bfloat16)


def start_kernel(
    count_ref, features_hbm, rows_hbm, cols_hbm, edges_ref, tiles_hbm, metas_ref, root_ref, gathered_ref,
    tiles_ref, features_ref, meta, lists, raw, slot_degree, degree, shares, roots,
    tile_sem, load_sem, list_sem, list_send, list_recv, meta_send, meta_recv, share_send, share_recv, root_send, root_recv, *sems,
):
    me = Place()
    peers = [lax.rem(me.col + i, 16) for i in range(1, 16)]
    across = me.col + 1 - 2 * me.core
    friends = [(lax.rem(me.row + i % 8, 8), me.col if i < 8 else across) for i in range(1, 16)]
    loads = [
        pltpu.make_async_copy(rows_hbm, meta.at[pl.ds(0, 8)], load_sem.at[0]),
        pltpu.make_async_copy(cols_hbm, meta.at[pl.ds(8, 8)], load_sem.at[1]),
        pltpu.make_async_copy(features_hbm, features_ref, load_sem.at[2]),
    ]
    own_lists = pltpu.make_async_copy(edges_ref.at[:, :, me.core], lists.at[me.core], list_sem)
    for load in loads:
        load.start()
    own_lists.start()
    meta[16:24, :] = jnp.full((8, TILE), count_ref[0, 0], jnp.int32)
    greet([(me.row, peer) for peer in peers] + [friend for i, friend in enumerate(friends) if i != 7])
    partner = me.at(core=1 - me.core)

    give_lists = pltpu.make_async_remote_copy(
        edges_ref.at[:, :, 1 - me.core], lists.at[me.core], list_send, list_recv, device_id=partner, device_id_type=MESH
    )
    give_meta = pltpu.make_async_remote_copy(
        meta, metas_ref.at[me.core], meta_send, meta_recv, device_id=partner, device_id_type=MESH
    )

    def tile_copy(bank):
        return pltpu.make_async_copy(tiles_ref.at[bank], tiles_hbm.at[bank], tile_sem.at[bank])

    def share_copy(i):
        return pltpu.make_async_remote_copy(
            degree.at[peers[i]], shares.at[i], share_send.at[i], share_recv.at[i],
            device_id=(me.row, peers[i]), device_id_type=MESH,
        )

    def root_copy(i):
        block = roots.at[me.core, me.y, me.x_lo]
        return pltpu.make_async_remote_copy(
            block, block, root_send.at[i], root_recv.at[i], device_id=friends[i], device_id_type=MESH
        )

    give_lists.start()
    for load in loads:
        load.wait()
    give_meta.start()
    metas_ref[me.core] = meta[...]

    def turn(k, carry):
        raw[me.core, me.y, me.x_lo, k] = wide(features_ref[k]).T.astype(jnp.bfloat16)
        return carry

    lax.fori_loop(0, 8, turn, 0)
    slot_degree[...] = jnp.zeros_like(slot_degree)
    stages, drain = spread_stages(me, raw, sems, RAW_CHUNK)
    ticks = len(stages) + RAW_CHUNK - 1
    groups = 2 * lists.shape[2] * 8 // GROUP
    blocks = GROUP // 8
    own_lists.wait()

    def build(group, carry):
        for tick, when in enumerate(TICK_GROUP):
            @pl.when(group == when)
            def _(tick=tick):
                for q in range(RAW_CHUNK):
                    if 0 <= tick - q < len(stages):
                        stages[tick - q](q)

        @pl.when(group == groups // 2)
        def _():
            give_lists.wait_recv()
            give_meta.wait_recv()

        half = group // (groups // 2)
        place = group % (groups // 2)
        owner = me.core + half * (1 - 2 * me.core)
        bank = owner * (groups // 2) + place
        base = place * blocks

        shape = (blocks, 8, TILE)
        slot = (lax.broadcasted_iota(jnp.int32, shape, 0) + base) * 16 + 8 * me.core + lax.broadcasted_iota(jnp.int32, shape, 1)
        live = slot < jnp.broadcast_to(metas_ref[owner, 16:17, :].reshape(1, 1, TILE), shape)
        dst = jnp.where(live, lists[owner, 0, pl.ds(base, blocks)], -1).reshape(GROUP, TILE)
        src = lists[owner, 1, pl.ds(base, blocks)].reshape(GROUP, TILE)
        dst, src = narrow(dst), narrow(src)
        cell = narrow(lax.broadcasted_iota(jnp.int32, (TILE, TILE), 0))
        for block in range(blocks):
            totals = []
            for i in range(8 * block, 8 * block + 8):
                counts = lax.dot_general(
                    hot(src[i : i + 1, :], cell), hot(dst[i : i + 1, :], cell), (((1,), (1,)), ((), ())),
                    preferred_element_type=jnp.float32,
                )
                tiles_ref[bank, i] = counts.astype(jnp.bfloat16)
                totals.append(jnp.sum(counts, axis=0, keepdims=True))
            slot_degree[owner, (base + block) * 2 + me.core] = jnp.concatenate(totals, axis=0)
        tile_copy(bank).start()
        return carry

    lax.fori_loop(0, groups, build, 0)

    cell = lax.broadcasted_iota(jnp.int32, (TILE, TILE), 0)
    counted = jnp.zeros((TILE, TILE), jnp.float32)
    for owner in range(2):
        for j in range(8):
            row_hot = (jnp.broadcast_to(metas_ref[owner, j : j + 1, :], (TILE, TILE)) == cell).astype(jnp.float32)
            slots = slot_degree[owner, 16 * j : 16 * j + 16].reshape(TILE, TILE)
            counted += jnp.dot(
                row_hot.astype(jnp.bfloat16), slots.astype(jnp.bfloat16), preferred_element_type=jnp.float32
            )
    degree[...] = counted.reshape(16, 8, TILE)
    for i in range(15):
        share_copy(i).start()
    for tick in range(len(TICK_GROUP), ticks):
        for q in range(RAW_CHUNK):
            if 0 <= tick - q < len(stages):
                stages[tick - q](q)
    total = degree[me.col]
    for i in range(15):
        share_copy(i).wait_recv()
        total = total + shares[i]
    root = lax.rsqrt(1.0 + total)
    root_ref[...] = root
    roots[me.core, me.y, me.x_lo] = root
    for i in range(15):
        root_copy(i).start()
    drain()
    for i in range(15):
        root_copy(i).wait_recv()

    def scale(i, carry):
        c, y, x, k = i // 64, (i // 16) % 4, (i // 8) % 2, i % 8
        gathered_ref[c, y, x, k] = (wide(raw[c, y, x, k]) * roots[c, y, x, pl.ds(k, 1), :]).astype(jnp.bfloat16)
        return carry

    lax.fori_loop(0, 128, scale, 0, unroll=4)
    for i in range(15):
        share_copy(i).wait_send()
        root_copy(i).wait_send()
    give_lists.wait_send()
    give_meta.wait_send()
    for bank in range(groups):
        tile_copy(bank).wait()


TICK_GROUP = (0, 4, 7, 10, 13)


def sum_kernel(spreads, part_ref, root_ref, hop_ref, *refs):
    me = Place()
    gathered_ref = refs[0] if spreads else None
    scratch = refs[1:] if spreads else refs
    greet(sum_devices(me) + (spread_devices(me) if spreads else []))

    def finish(k, total):
        root = root_ref[pl.ds(k, 1), :]
        hop_ref[k] = (total * root).T.astype(jnp.bfloat16)
        if spreads:
            gathered_ref[me.core, me.y, me.x_lo, k] = (total * (root * root)).astype(jnp.bfloat16)

    begin, stages, drain = sum_stages(me, part_ref, scratch[:6], scratch[6:N_SUM], finish)
    begin()
    if spreads:
        more, drain_spread = spread_stages(me, gathered_ref, scratch[N_SUM:], SUM_CHUNK)
        run_stages(stages + more, SUM_LAGS, SUM_CHUNK)
        drain_spread()
    else:
        run_stages(stages, SUM_LAGS[:4], SUM_CHUNK)
    drain()


VMEM = pl.BlockSpec(memory_space=pltpu.VMEM)
SMEM = pl.BlockSpec(memory_space=pltpu.SMEM)
HBM = pl.BlockSpec(memory_space=pltpu.HBM)
GATHERED = (2, 4, 2, 8, TILE, TILE)


def comm_params(number, limit):
    return pltpu.CompilerParams(collective_id=number, has_side_effects=True, vmem_limit_bytes=limit)


def start(counts, features, rows, cols, edges):
    dma = pltpu.SemaphoreType.DMA
    slots = edges.shape[1]
    shape = jax.ShapeDtypeStruct
    f32, bf16, i32 = jnp.float32, jnp.bfloat16, jnp.int32
    return pl.pallas_call(
        start_kernel,
        out_shape=[
            shape((slots // GROUP, GROUP, TILE, TILE), bf16), shape((2, 24, TILE), i32), shape((8, TILE), f32), shape(GATHERED, bf16)
        ],
        in_specs=[SMEM, HBM, HBM, HBM, HBM],
        out_specs=[HBM, VMEM, VMEM, VMEM],
        scratch_shapes=[
            pltpu.VMEM((slots // GROUP, GROUP, TILE, TILE), bf16),
            pltpu.VMEM((8, TILE, TILE), bf16),
            pltpu.VMEM((24, TILE), i32),
            pltpu.VMEM((2, 2, slots // 16, 8, TILE), i32),
            pltpu.VMEM(GATHERED, bf16),
            pltpu.VMEM((2, slots // 8, 8, TILE), f32),
            pltpu.VMEM((16, 8, TILE), f32),
            pltpu.VMEM((15, 8, TILE), f32),
            pltpu.VMEM((2, 4, 2, 8, TILE), f32),
            dma((slots // GROUP,)), dma((3,)), *[dma] * 5, *[dma((15,))] * 4,
            *spread_scratch(RAW_CHUNK),
        ],
        compiler_params=comm_params(0, START_LIMIT),
        name="start_build",
    )(
        counts, features.reshape(8, TILE, TILE), rows.reshape(8, TILE), cols.reshape(8, TILE),
        edges.reshape(2, slots // 16, 2, 8, TILE),
    )


def live_count(metas_ref, core, owner):
    count = metas_ref[owner, 16, 0]
    return count // 16 * 8 + jnp.clip(count % 16 - 8 * core, 0, 8)


def apply_kernel(metas_ref, tiles_hbm, x_ref, total, tiles_ref, tile_sem):
    core = lax.axis_index("col") % 2
    half_groups = tiles_ref.shape[0] // 2
    live = [(live_count(metas_ref, core, owner) + GROUP - 1) // GROUP for owner in range(2)]

    def tile_copy(bank):
        return pltpu.make_async_copy(tiles_hbm.at[bank], tiles_ref.at[bank], tile_sem.at[bank])

    for owner in range(2):
        def fetch(place, carry, owner=owner):
            tile_copy(owner * half_groups + place).start()
            return carry

        lax.fori_loop(0, live[owner], fetch, 0)
    total[...] = jnp.zeros_like(total)
    for owner in range(2):
        def apply_group(place, carry, owner=owner):
            base = place * GROUP * 2 + 8 * core
            tile_copy(owner * half_groups + place).wait()
            for start in range(0, GROUP, BATCH):
                slots = [base + i // 8 * 16 + i % 8 for i in range(start, start + BATCH)]
                products = [
                    jnp.dot(
                        x_ref[owner * 64 + metas_ref[owner, 8 + slot // 128, slot % 128]],
                        tiles_ref[owner * half_groups + place, start + j],
                        preferred_element_type=jnp.float32,
                    )
                    for j, slot in enumerate(slots)
                ]
                for slot, product in zip(slots, products):
                    total[metas_ref[owner, slot // 128, slot % 128]] += product
            return carry

        lax.fori_loop(0, live[owner], apply_group, 0)


def apply_tiles(metas, tiles, x):
    return pl.pallas_call(
        apply_kernel,
        in_specs=[SMEM, HBM, VMEM],
        out_specs=VMEM,
        scratch_shapes=[pltpu.VMEM(tiles.shape, tiles.dtype), pltpu.SemaphoreType.DMA((tiles.shape[0],))],
        out_shape=jax.ShapeDtypeStruct((TILE, TILE, TILE), jnp.float32),
        compiler_params=pltpu.CompilerParams(vmem_limit_bytes=APPLY_LIMIT),
        name="apply_tiles",
    )(metas, tiles, x)


def sum_parts(part, root, spreads):
    hop = jax.ShapeDtypeStruct((8, TILE, TILE), jnp.bfloat16)
    gathered = jax.ShapeDtypeStruct(GATHERED, jnp.bfloat16)
    return pl.pallas_call(
        functools.partial(sum_kernel, spreads),
        out_shape=[hop, gathered] if spreads else [hop],
        in_specs=[VMEM, VMEM],
        out_specs=[VMEM, VMEM] if spreads else [VMEM],
        scratch_shapes=sum_scratch() + (spread_scratch(SUM_CHUNK) if spreads else []),
        compiler_params=comm_params(1 if spreads else 2, SUM_LIMIT),
        name="sum_spread" if spreads else "sum_last",
    )(part.reshape(2, 4, 2, 8, TILE, TILE), root)


def local(features, tile_rows, tile_cols, edge_lists, tile_counts):
    edges = edge_lists.reshape(2, *edge_lists.shape[3:])
    tiles, metas, root, gathered = start(tile_counts, features, tile_rows, tile_cols, edges)
    part = apply_tiles(metas, tiles, gathered.reshape(128, TILE, TILE))
    hop_one, gathered = sum_parts(part, root, True)
    part = apply_tiles(metas, tiles, gathered.reshape(128, TILE, TILE))
    (hop_two,) = sum_parts(part, root, False)
    return (hop_one.reshape(features.shape), hop_two.reshape(features.shape))


def solution(mesh):
    placed = (
        P(("row", "col"), None),
        P("row", "col", None),
        P("row", "col", None),
        P(None, "row", "col", None, None),
        P("row", "col"),
    )
    return jax.shard_map(
        local,
        mesh=mesh,
        in_specs=placed,
        out_specs=(P(("row", "col"), None), P(("row", "col"), None)),
        check_vma=False,
    )
```

profile of v0, /device:TPU:0, one launch (start us, length us, event | category | flops | bytes accessed | tf_op | source)
XLA Modules:
  0.0 147.7 jit_solution(6884607106798568862)
XLA Ops:
  1.3 0.0 copy-start
  1.3 1.2 copy-done
  2.5 0.0 copy-start.1
  2.5 0.9 copy-done.1
  3.5 0.0 copy-start.2
  3.5 0.7 copy-done.2
  4.1 0.0 copy-start.3
  4.1 0.7 copy-done.3
  4.8 48.6 %start_build.1 = (bf16[16,64,128,128]{3,2,1,0:T(8,128)(2,1)}, s32[2,24,128]{2,1,0:T(8,128)S(1)}, f32[8,128]{1,0:T(8,128)S(1)}, bf16[2,4,2,8,128,128]{5,4,3,2,1,0:T(8,128)(2,1)S(1)}) custom-call(s32[1,1]{1,0:T(1,128)S(6)} %copy.9.count_ref, bf16[8,128,128]{2,1,0:T(8,128)(2,1)S(1)} %bitcast.16, s32[8,128]{1,0:T(8,128)S(1)} %bitcast.18, s32[8,128]{1,0:T(8,128)S(1)} %bitcast.19, ...), custom_call_target="tpu_custom_call" | custom-call | tf_op jit(solution)/shard_map/start_build/pallas_call | solution.py:452
  53.4 7.1 %apply_tiles.2 = f32[128,128,128]{2,1,0:T(8,128)S(1)} custom-call(s32[2,24,128]{2,1,0:T(8,128)S(1)} %get-tuple-element.8.metas_ref, bf16[16,64,128,128]{3,2,1,0:T(8,128)(2,1)} %get-tuple-element.9.tiles_hbm, bf16[128,128,128]{2,1,0:T(8,128)(2,1)S(1)} %bitcast.12), custom_call_target="tpu_custom_call" | custom-call | tf_op jit(solution)/shard_map/apply_tiles/pallas_call | solution.py:522
  60.5 46.6 %sum_spread.1 = (bf16[8,128,128]{2,1,0:T(8,128)(2,1)S(1)}, bf16[2,4,2,8,128,128]{5,4,3,2,1,0:T(8,128)(2,1)S(1)}) custom-call(f32[2,4,2,8,128,128]{5,4,3,2,1,0:T(8,128)S(1)} %bitcast.11, f32[8,128]{1,0:T(8,128)S(1)} %get-tuple-element.11.root_ref), custom_call_target="tpu_custom_call" | custom-call | tf_op jit(solution)/shard_map/sum_spread/pallas_call | solution.py:536
  107.0 7.1 %apply_tiles.3 = f32[128,128,128]{2,1,0:T(8,128)S(1)} custom-call(s32[2,24,128]{2,1,0:T(8,128)S(1)} %get-tuple-element.8.metas_ref, bf16[16,64,128,128]{3,2,1,0:T(8,128)(2,1)} %get-tuple-element.9.tiles_hbm, bf16[128,128,128]{2,1,0:T(8,128)(2,1)S(1)} %bitcast.13), custom_call_target="tpu_custom_call" | custom-call | tf_op jit(solution)/shard_map/apply_tiles/pallas_call | solution.py:522
  114.1 32.2 %sum_last.1 = bf16[8,128,128]{2,1,0:T(8,128)(2,1)S(1)} custom-call(f32[2,4,2,8,128,128]{5,4,3,2,1,0:T(8,128)S(1)} %bitcast.10, f32[8,128]{1,0:T(8,128)S(1)} %get-tuple-element.11.root_ref), custom_call_target="tpu_custom_call" | custom-call | tf_op jit(solution)/shard_map/sum_last/pallas_call | solution.py:536
  146.3 0.7 copy.10
  147.0 0.7 copy.11
Async XLA Ops:
  1.3 1.2 copy-start
  2.5 0.9 copy-start.1
  3.5 0.7 copy-start.2
  4.1 0.7 copy-start.3
where the time goes:
time: 149 us; the launch traced here: 148 us
  Pallas kernels  141 us (95%)
  local copies, waits for them, and re-layouts  4.95 us (3%)
    pallas_call x2, Pallas kernels, sum_parts(): pl.pallas_call(functools.partial(sum_kernel, spreads), out_shape=[hop, ga...  78.7 us
    pallas_call x1, Pallas kernels, start(): pl.pallas_call(start_kernel, out_shape=[shape((slots // GROUP, GROUP, TIL...  48.6 us
    pallas_call x2, Pallas kernels, apply_tiles(): pl.pallas_call(apply_kernel, in_specs=[SMEM, HBM, VMEM], out_specs=VMEM,...  14.1 us
    unnamed x10, local copies, waits for them, and re-layouts  4.95 us

commit v1 on v0

--- a/solution.py
+++ b/solution.py
@@ -318,18 +318,16 @@
     lax.fori_loop(0, 8, turn, 0)
     slot_degree[...] = jnp.zeros_like(slot_degree)
     stages, drain = spread_stages(me, raw, sems, RAW_CHUNK)
-    ticks = len(stages) + RAW_CHUNK - 1
     groups = 2 * lists.shape[2] * 8 // GROUP
     blocks = GROUP // 8
     own_lists.wait()
 
     def build(group, carry):
-        for tick, when in enumerate(TICK_GROUP):
+        for when, moves in RAW_MOVES:
             @pl.when(group == when)
-            def _(tick=tick):
-                for q in range(RAW_CHUNK):
-                    if 0 <= tick - q < len(stages):
-                        stages[tick - q](q)
+            def _(moves=moves):
+                for stage, q in moves:
+                    stages[stage](q)
 
         @pl.when(group == groups // 2)
         def _():
@@ -353,7 +351,7 @@
             totals = []
             for i in range(8 * block, 8 * block + 8):
                 counts = lax.dot_general(
-                    hot(src[i : i + 1, :], cell), hot(dst[i : i + 1, :], cell), (((1,), (1,)), ((), ())),
+                    hot(src[i : i + 1, :], cell), hot(dst[i : i + 1, :], cell).astype(jnp.float8_e4m3fn), (((1,), (1,)), ((), ())),
                     preferred_element_type=jnp.float32,
                 )
                 tiles_ref[bank, i] = counts.astype(jnp.bfloat16)
@@ -376,10 +374,8 @@
     degree[...] = counted.reshape(16, 8, TILE)
     for i in range(15):
         share_copy(i).start()
-    for tick in range(len(TICK_GROUP), ticks):
-        for q in range(RAW_CHUNK):
-            if 0 <= tick - q < len(stages):
-                stages[tick - q](q)
+    for stage, q in RAW_LATE:
+        stages[stage](q)
     total = degree[me.col]
     for i in range(15):
         share_copy(i).wait_recv()
@@ -389,6 +385,8 @@
     roots[me.core, me.y, me.x_lo] = root
     for i in range(15):
         root_copy(i).start()
+    for q in range(RAW_CHUNK):
+        stages[4](q)
     drain()
     for i in range(15):
         root_copy(i).wait_recv()
@@ -408,7 +406,13 @@
         tile_copy(bank).wait()
 
 
-TICK_GROUP = (0, 4, 7, 10, 13)
+RAW_MOVES = (
+    (0, ((0, 0), (0, 1))),
+    (6, ((1, 0), (2, 0))),
+    (10, ((1, 1), (2, 1))),
+    (14, ((3, 0),)),
+)
+RAW_LATE = ((3, 1),)
 
 
 def sum_kernel(spreads, part_ref, root_ref, hop_ref, *refs):

time: 149 us -> 135 us (0.906)
  Pallas kernels: 141 us -> 128 us
    pallas_call x1, Pallas kernels: 48.6 us -> 34.8 us  [start(): pl.pallas_call(start_kernel, out_shape=[shape((slots // GROUP, GROUP, TIL...]
where the time goes in v1:
time: 135 us; the launch traced here: 134 us
  Pallas kernels  128 us (95%)
  local copies, waits for them, and re-layouts  4.95 us (4%)
    pallas_call x2, Pallas kernels, sum_parts(): pl.pallas_call(functools.partial(sum_kernel, spreads), out_shape=[hop, ga...  79.1 us
    pallas_call x1, Pallas kernels, start(): pl.pallas_call(start_kernel, out_shape=[shape((slots // GROUP, GROUP, TIL...  34.8 us
    pallas_call x2, Pallas kernels, apply_tiles(): pl.pallas_call(apply_kernel, in_specs=[SMEM, HBM, VMEM], out_specs=VMEM,...  14.1 us
    unnamed x10, local copies, waits for them, and re-layouts  4.95 us

profile of v1, /device:TPU:0, one launch (start us, length us, event | category | flops | bytes accessed | tf_op | source)
XLA Modules:
  0.0 134.3 jit_solution(7629065913809532245)
XLA Ops:
  1.3 0.0 copy-start
  1.3 1.2 copy-done
  2.5 0.0 copy-start.1
  2.5 0.9 copy-done.1
  3.5 0.0 copy-start.2
  3.5 0.7 copy-done.2
  4.1 0.0 copy-start.3
  4.1 0.7 copy-done.3
  4.8 34.8 %start_build.1 = (bf16[16,64,128,128]{3,2,1,0:T(8,128)(2,1)}, s32[2,24,128]{2,1,0:T(8,128)S(1)}, f32[8,128]{1,0:T(8,128)S(1)}, bf16[2,4,2,8,128,128]{5,4,3,2,1,0:T(8,128)(2,1)S(1)}) custom-call(s32[1,1]{1,0:T(1,128)S(6)} %copy.9.count_ref, bf16[8,128,128]{2,1,0:T(8,128)(2,1)S(1)} %bitcast.16, s32[8,128]{1,0:T(8,128)S(1)} %bitcast.18, s32[8,128]{1,0:T(8,128)S(1)} %bitcast.19, ...), custom_call_target="tpu_custom_call" | custom-call | tf_op jit(solution)/shard_map/start_build/pallas_call | solution.py:456
  39.6 7.1 %apply_tiles.2 = f32[128,128,128]{2,1,0:T(8,128)S(1)} custom-call(s32[2,24,128]{2,1,0:T(8,128)S(1)} %get-tuple-element.8.metas_ref, bf16[16,64,128,128]{3,2,1,0:T(8,128)(2,1)} %get-tuple-element.9.tiles_hbm, bf16[128,128,128]{2,1,0:T(8,128)(2,1)S(1)} %bitcast.12), custom_call_target="tpu_custom_call" | custom-call | tf_op jit(solution)/shard_map/apply_tiles/pallas_call | solution.py:526
  46.7 48.4 %sum_spread.1 = (bf16[8,128,128]{2,1,0:T(8,128)(2,1)S(1)}, bf16[2,4,2,8,128,128]{5,4,3,2,1,0:T(8,128)(2,1)S(1)}) custom-call(f32[2,4,2,8,128,128]{5,4,3,2,1,0:T(8,128)S(1)} %bitcast.11, f32[8,128]{1,0:T(8,128)S(1)} %get-tuple-element.11.root_ref), custom_call_target="tpu_custom_call" | custom-call | tf_op jit(solution)/shard_map/sum_spread/pallas_call | solution.py:540
  95.1 7.1 %apply_tiles.3 = f32[128,128,128]{2,1,0:T(8,128)S(1)} custom-call(s32[2,24,128]{2,1,0:T(8,128)S(1)} %get-tuple-element.8.metas_ref, bf16[16,64,128,128]{3,2,1,0:T(8,128)(2,1)} %get-tuple-element.9.tiles_hbm, bf16[128,128,128]{2,1,0:T(8,128)(2,1)S(1)} %bitcast.13), custom_call_target="tpu_custom_call" | custom-call | tf_op jit(solution)/shard_map/apply_tiles/pallas_call | solution.py:526
  102.2 30.7 %sum_last.1 = bf16[8,128,128]{2,1,0:T(8,128)(2,1)S(1)} custom-call(f32[2,4,2,8,128,128]{5,4,3,2,1,0:T(8,128)S(1)} %bitcast.10, f32[8,128]{1,0:T(8,128)S(1)} %get-tuple-element.11.root_ref), custom_call_target="tpu_custom_call" | custom-call | tf_op jit(solution)/shard_map/sum_last/pallas_call | solution.py:540
  132.9 0.7 copy.10
  133.6 0.7 copy.11
Async XLA Ops:
  1.3 1.2 copy-start
  2.5 0.9 copy-start.1
  3.5 0.7 copy-start.2
  4.1 0.7 copy-start.3

commit v2 on v1

--- a/solution.py
+++ b/solution.py
@@ -388,15 +388,20 @@
     for q in range(RAW_CHUNK):
         stages[4](q)
     drain()
-    for i in range(15):
-        root_copy(i).wait_recv()
-
-    def scale(i, carry):
-        c, y, x, k = i // 64, (i // 16) % 4, (i // 8) % 2, i % 8
-        gathered_ref[c, y, x, k] = (wide(raw[c, y, x, k]) * roots[c, y, x, pl.ds(k, 1), :]).astype(jnp.bfloat16)
-        return carry
-
-    lax.fori_loop(0, 128, scale, 0, unroll=4)
+
+    def scale_block(c, row):
+        y, x = row // 2, row % 2
+
+        def scale(k, carry):
+            gathered_ref[c, y, x, k] = (wide(raw[c, y, x, k]) * roots[c, y, x, pl.ds(k, 1), :]).astype(jnp.bfloat16)
+            return carry
+
+        lax.fori_loop(0, 8, scale, 0, unroll=4)
+
+    scale_block(me.core, me.row)
+    for i in (8, 2, 6, 10, 14, 1, 7, 9, 15, 3, 5, 11, 13, 4, 12):
+        root_copy(i - 1).wait_recv()
+        scale_block(me.core if i < 8 else 1 - me.core, lax.rem(me.row + 8 - i % 8, 8))
     for i in range(15):
         share_copy(i).wait_send()
         root_copy(i).wait_send()
@@ -486,7 +491,13 @@
     return count // 16 * 8 + jnp.clip(count % 16 - 8 * core, 0, 8)
 
 
-def apply_kernel(metas_ref, tiles_hbm, x_ref, total, tiles_ref, tile_sem):
+def apply_kernel(carries, metas_ref, tiles_hbm, x_ref, *refs):
+    if carries:
+        carried, total, carried_out, tiles_ref, tile_sem, carry_sem = refs
+        carry_copy = pltpu.make_async_copy(carried, carried_out, carry_sem)
+        carry_copy.start()
+    else:
+        total, tiles_ref, tile_sem = refs
     core = lax.axis_index("col") % 2
     half_groups = tiles_ref.shape[0] // 2
     live = [(live_count(metas_ref, core, owner) + GROUP - 1) // GROUP for owner in range(2)]
@@ -503,35 +514,39 @@
     total[...] = jnp.zeros_like(total)
     for owner in range(2):
         def apply_group(place, carry, owner=owner):
-            base = place * GROUP * 2 + 8 * core
-            tile_copy(owner * half_groups + place).wait()
+            bank = owner * half_groups + place
+            tile_copy(bank).wait()
             for start in range(0, GROUP, BATCH):
-                slots = [base + i // 8 * 16 + i % 8 for i in range(start, start + BATCH)]
+                lanes = [8 * core + (i // 8 * 16 + i % 8) for i in range(start, start + BATCH)]
                 products = [
                     jnp.dot(
-                        x_ref[owner * 64 + metas_ref[owner, 8 + slot // 128, slot % 128]],
-                        tiles_ref[owner * half_groups + place, start + j],
+                        x_ref[owner * 64 + metas_ref[owner, 8 + place, lane]],
+                        tiles_ref[bank, start + j],
                         preferred_element_type=jnp.float32,
                     )
-                    for j, slot in enumerate(slots)
+                    for j, lane in enumerate(lanes)
                 ]
-                for slot, product in zip(slots, products):
-                    total[metas_ref[owner, slot // 128, slot % 128]] += product
+                for lane, product in zip(lanes, products):
+                    total[metas_ref[owner, place, lane]] += product
             return carry
 
         lax.fori_loop(0, live[owner], apply_group, 0)
-
-
-def apply_tiles(metas, tiles, x):
+    if carries:
+        carry_copy.wait()
+
+
+def apply_tiles(metas, tiles, x, *carried):
+    total = jax.ShapeDtypeStruct((TILE, TILE, TILE), jnp.float32)
+    dma = pltpu.SemaphoreType.DMA
     return pl.pallas_call(
-        apply_kernel,
-        in_specs=[SMEM, HBM, VMEM],
-        out_specs=VMEM,
-        scratch_shapes=[pltpu.VMEM(tiles.shape, tiles.dtype), pltpu.SemaphoreType.DMA((tiles.shape[0],))],
-        out_shape=jax.ShapeDtypeStruct((TILE, TILE, TILE), jnp.float32),
+        functools.partial(apply_kernel, len(carried)),
+        in_specs=[SMEM, HBM, VMEM] + [VMEM] * len(carried),
+        out_specs=[VMEM] + [HBM] * len(carried),
+        scratch_shapes=[pltpu.VMEM(tiles.shape, tiles.dtype), dma((tiles.shape[0],))] + [dma] * len(carried),
+        out_shape=[total] + [jax.ShapeDtypeStruct(c.shape, c.dtype) for c in carried],
         compiler_params=pltpu.CompilerParams(vmem_limit_bytes=APPLY_LIMIT),
         name="apply_tiles",
-    )(metas, tiles, x)
+    )(metas, tiles, x, *carried)
 
 
 def sum_parts(part, root, spreads):
@@ -551,9 +566,9 @@
 def local(features, tile_rows, tile_cols, edge_lists, tile_counts):
     edges = edge_lists.reshape(2, *edge_lists.shape[3:])
     tiles, metas, root, gathered = start(tile_counts, features, tile_rows, tile_cols, edges)
-    part = apply_tiles(metas, tiles, gathered.reshape(128, TILE, TILE))
+    (part,) = apply_tiles(metas, tiles, gathered.reshape(128, TILE, TILE))
     hop_one, gathered = sum_parts(part, root, True)
-    part = apply_tiles(metas, tiles, gathered.reshape(128, TILE, TILE))
+    part, hop_one = apply_tiles(metas, tiles, gathered.reshape(128, TILE, TILE), hop_one)
     (hop_two,) = sum_parts(part, root, False)
     return (hop_one.reshape(features.shape), hop_two.reshape(features.shape))
 

time: 135 us -> 132 us (0.978); the launches traced: 134 us -> 130 us
  Pallas kernels: 128 us -> 124 us
    pallas_call x1, Pallas kernels: 34.8 us -> 32.4 us  [start(): pl.pallas_call(start_kernel, out_shape=[shape((slots // GROUP, GROUP, TIL...]
    pallas_call x2, Pallas kernels: 14.1 us -> 12.5 us  [apply_tiles(): pl.pallas_call(functools.partial(apply_kernel, len(carried)), in_specs=[S...]
    unnamed x10 -> x9, local copies, waits for them, and re-layouts: 4.95 us -> 4.25 us
where the time goes in v2:
time: 132 us; the launch traced here: 130 us
  Pallas kernels  124 us (94%)
  local copies, waits for them, and re-layouts  4.25 us (3%)
  between operations  1.33 us (1%)
    pallas_call x2, Pallas kernels, sum_parts(): pl.pallas_call(functools.partial(sum_kernel, spreads), out_shape=[hop, ga...  79.4 us
    pallas_call x1, Pallas kernels, start(): pl.pallas_call(start_kernel, out_shape=[shape((slots // GROUP, GROUP, TIL...  32.4 us
    pallas_call x2, Pallas kernels, apply_tiles(): pl.pallas_call(functools.partial(apply_kernel, len(carried)), in_specs=[S...  12.5 us
    unnamed x9, local copies, waits for them, and re-layouts  4.25 us

profile of v2, /device:TPU:0, one launch (start us, length us, event | category | flops | bytes accessed | tf_op | source)
XLA Modules:
  0.0 129.9 jit_solution(3365726881731323414)
XLA Ops:
  1.3 0.0 copy-start
  1.3 1.2 copy-done
  2.5 0.0 copy-start.1
  2.5 0.9 copy-done.1
  3.5 0.0 copy-start.2
  3.5 0.7 copy-done.2
  4.1 0.0 copy-start.3
  4.1 0.7 copy-done.3
  4.8 32.4 %start_build.1 = (bf16[16,64,128,128]{3,2,1,0:T(8,128)(2,1)}, s32[2,24,128]{2,1,0:T(8,128)S(1)}, f32[8,128]{1,0:T(8,128)S(1)}, bf16[2,4,2,8,128,128]{5,4,3,2,1,0:T(8,128)(2,1)S(1)}) custom-call(s32[1,1]{1,0:T(1,128)S(6)} %copy.8.count_ref, bf16[8,128,128]{2,1,0:T(8,128)(2,1)S(1)} %bitcast.16, s32[8,128]{1,0:T(8,128)S(1)} %bitcast.17, s32[8,128]{1,0:T(8,128)S(1)} %bitcast.18, ...), custom_call_target="tpu_custom_call" | custom-call | tf_op jit(solution)/shard_map/start_build/pallas_call | solution.py:461
  37.3 6.2 %apply_tiles.2 = f32[128,128,128]{2,1,0:T(8,128)S(1)} custom-call(s32[2,24,128]{2,1,0:T(8,128)S(1)} %get-tuple-element.10.metas_ref, bf16[16,64,128,128]{3,2,1,0:T(8,128)(2,1)} %get-tuple-element.11.tiles_hbm, bf16[128,128,128]{2,1,0:T(8,128)(2,1)S(1)} %bitcast.13), custom_call_target="tpu_custom_call" | custom-call | tf_op jit(solution)/shard_map/apply_tiles/pallas_call | solution.py:541
  43.5 48.8 %sum_spread.1 = (bf16[8,128,128]{2,1,0:T(8,128)(2,1)S(1)}, bf16[2,4,2,8,128,128]{5,4,3,2,1,0:T(8,128)(2,1)S(1)}) custom-call(f32[2,4,2,8,128,128]{5,4,3,2,1,0:T(8,128)S(1)} %bitcast.10, f32[8,128]{1,0:T(8,128)S(1)} %get-tuple-element.13.root_ref), custom_call_target="tpu_custom_call" | custom-call | tf_op jit(solution)/shard_map/sum_spread/pallas_call | solution.py:555
  92.2 6.3 %apply_tiles.3 = (f32[128,128,128]{2,1,0:T(8,128)S(1)}, bf16[8,128,128]{2,1,0:T(8,128)(2,1)}) custom-call(s32[2,24,128]{2,1,0:T(8,128)S(1)} %get-tuple-element.10.metas_ref, bf16[16,64,128,128]{3,2,1,0:T(8,128)(2,1)} %get-tuple-element.11.tiles_hbm, bf16[128,128,128]{2,1,0:T(8,128)(2,1)S(1)} %bitcast.12, bf16[8,128,128]{2,1,0:T(8,128)(2,1)S(1)} %get-tuple-element.15.refs_0_), custom_call_target="tpu_custom_call" | custom-call | tf_op jit(solution)/shard_map/apply_tiles/pallas_call | solution.py:541
  98.5 30.7 %sum_last.1 = bf16[8,128,128]{2,1,0:T(8,128)(2,1)S(1)} custom-call(f32[2,4,2,8,128,128]{5,4,3,2,1,0:T(8,128)S(1)} %bitcast.11, f32[8,128]{1,0:T(8,128)S(1)} %get-tuple-element.13.root_ref), custom_call_target="tpu_custom_call" | custom-call | tf_op jit(solution)/shard_map/sum_last/pallas_call | solution.py:555
  129.2 0.7 copy.9
Async XLA Ops:
  1.3 1.2 copy-start
  2.5 0.9 copy-start.1
  3.5 0.7 copy-start.2
  4.1 0.7 copy-start.3

commit v3 on v2

--- a/solution.py
+++ b/solution.py
@@ -79,35 +79,43 @@
     return x.astype(jnp.float32)
 
 
+ALL, BOTH = slice(None), pl.ds(1, 2)
+
+
 def sum_stages(me, part, bufs, sems, finish):
     given, running, arrived, kept, across, crossed = bufs
-    pair_send, pair_recv, ring_send, ring_recv, far_send, far_recv = sems
+    pair_send, pair_recv, ring_send, head_recv, tail_recv, far_send, far_recv = sems
     chunks = SUM_CHUNK
-
-    def pair_copy(q):
+    size = 8 // chunks
+    whole = pl.ds(0, 8)
+
+    def cut(q):
+        return span(q, chunks)
+
+    def pair_copy(where):
         return pltpu.make_async_remote_copy(
-            part.at[:, :, 1 - me.core, span(q, chunks)], given.at[:, :, span(q, chunks)],
-            pair_send.at[q], pair_recv.at[q],
+            part.at[:, :, 1 - me.core, where], given.at[:, :, where], pair_send, pair_recv.at[where.start // size],
             device_id=me.at(core=1 - me.core), device_id_type=MESH,
         )
 
-    def ring_copy(half, step, q):
-        up = (half == 0) == (step < 2)
+    def ring_copy(half, step, where):
+        q = where.start // size
+        up = True if half == ALL else (half == 0) == (step != 2)
         return pltpu.make_async_remote_copy(
-            running.at[half, step, span(q, chunks)], arrived.at[half, step, span(q, chunks)],
-            ring_send.at[half, step, q], ring_recv.at[half, step, q],
+            running.at[half, step, where], arrived.at[half, step, where],
+            ring_send, head_recv.at[q] if step == 0 else tail_recv.at[0 if half == ALL else half, q],
             device_id=me.at(z=(me.z + (1 if up else 3)) % 4), device_id_type=MESH,
         )
 
-    def far_copy(q):
+    def far_copy(where):
         return pltpu.make_async_remote_copy(
-            across.at[span(q, chunks)], crossed.at[span(q, chunks)], far_send.at[q], far_recv.at[q],
+            across.at[where], crossed.at[where], far_send, far_recv.at[where.start // size],
             device_id=me.at(x_hi=1 - me.x_hi), device_id_type=MESH,
         )
 
     def begin():
         for q in range(chunks):
-            pair_copy(q).start()
+            pair_copy(cut(q)).start()
 
     def local_sum(half, offset, k):
         x_hi = me.x_hi if half == 0 else 1 - me.x_hi
@@ -115,29 +123,28 @@
         return part[x_hi, z, me.core, k] + given[x_hi, z, k]
 
     def first(q):
-        pair_copy(q).wait_recv()
+        pair_copy(cut(q)).wait_recv()
         for step, offset in ((0, 2), (2, 3)):
             for half in (1, 0):
                 def body(k, half=half, step=step, offset=offset):
                     running[half, step, k] = local_sum(half, offset, k).astype(jnp.bfloat16)
 
                 each_tile(q, chunks, body)
-                ring_copy(half, step, q).start()
+                ring_copy(half, step, cut(q)).start()
 
     def middle(q):
+        ring_copy(ALL, 0, cut(q)).wait_recv()
         for half in (1, 0):
-            ring_copy(half, 0, q).wait_recv()
 
             def body(k, half=half):
                 running[half, 1, k] = (local_sum(half, 1, k) + wide(arrived[half, 0, k])).astype(jnp.bfloat16)
 
             each_tile(q, chunks, body)
-            ring_copy(half, 1, q).start()
+            ring_copy(half, 1, cut(q)).start()
 
     def last(q):
         for half in (1, 0):
-            ring_copy(half, 2, q).wait_recv()
-            ring_copy(half, 1, q).wait_recv()
+            ring_copy(half, BOTH, cut(q)).wait_recv()
 
             def body(k, half=half):
                 total = local_sum(half, 0, k) + (wide(arrived[half, 1, k]) + wide(arrived[half, 2, k]))
@@ -148,19 +155,16 @@
 
             each_tile(q, chunks, body)
             if half == 1:
-                far_copy(q).start()
+                far_copy(cut(q)).start()
 
     def done(q):
-        far_copy(q).wait_recv()
+        far_copy(cut(q)).wait_recv()
         each_tile(q, chunks, lambda k: finish(k, kept[k] + wide(crossed[k])))
 
     def drain():
-        for q in range(chunks):
-            pair_copy(q).wait_send()
-            far_copy(q).wait_send()
-            for half in (0, 1):
-                for step in range(3):
-                    ring_copy(half, step, q).wait_send()
+        pair_copy(whole).wait_send()
+        far_copy(whole).wait_send()
+        ring_copy(ALL, ALL, whole).wait_send()
 
     return begin, [first, middle, last, done], drain
 
@@ -169,15 +173,16 @@
     block = lambda *lead, dtype=jnp.bfloat16: pltpu.VMEM((*lead, 8, TILE, TILE), dtype)
     dma = pltpu.SemaphoreType.DMA
     bufs = [block(2, 4, dtype=jnp.float32), block(2, 3), block(2, 3), block(dtype=jnp.float32), block(), block()]
-    sems = [dma((SUM_CHUNK,))] * 2 + [dma((2, 3, SUM_CHUNK))] * 2 + [dma((SUM_CHUNK,))] * 2
+    each = dma((SUM_CHUNK,))
+    sems = [dma, each, dma, each, dma((2, SUM_CHUNK)), dma, each]
     return bufs + sems
 
 
-N_SUM = 12
+N_SUM = 13
 
 
 def spread_stages(me, gathered, sems, chunks):
-    side_send, side_recv, near_send, near_recv, relay_send, relay_recv, pass_send, pass_recv = sems
+    side_send, near_send, relay_send, pass_send, side_recv, own_recv, beside_recv, rest_recv, pass_recv = sems
 
     def copy(block, send, recv, device):
         return pltpu.make_async_remote_copy(block, block, send, recv, device_id=device, device_id_type=MESH)
@@ -185,19 +190,23 @@
     def block(y, x_lo, q):
         return gathered.at[me.core, (me.y + y) % 4, me.x_lo if x_lo == 0 else 1 - me.x_lo, span(q, chunks)]
 
+    def along(way):
+        return me.at(y=(me.y + (1 if way == 0 else 3)) % 4)
+
+    beside_device, other_core = me.at(x_lo=1 - me.x_lo), me.at(core=1 - me.core)
+
     def side_copy(q):
-        return copy(block(0, 0, q), side_send.at[q], side_recv.at[q], me.at(x_lo=1 - me.x_lo))
+        return copy(block(0, 0, q), side_send, side_recv.at[q], beside_device)
 
     def near_copy(kind, way, q):
-        device = me.at(y=(me.y + (1 if way == 0 else 3)) % 4)
-        return copy(block(0, kind, q), near_send.at[kind, way, q], near_recv.at[kind, way, q], device)
+        recv = rest_recv if kind != way else own_recv if kind == 0 else beside_recv
+        return copy(block(0, kind, q), near_send, recv.at[q], along(way))
 
     def relay_copy(way, q):
-        device = me.at(y=(me.y + (1 if way == 0 else 3)) % 4)
-        return copy(block(3 if way == 0 else 1, way, q), relay_send.at[way, q], relay_recv.at[way, q], device)
+        return copy(block(3 if way == 0 else 1, way, q), relay_send, rest_recv.at[q], along(way))
 
     def pass_copy(y, x_lo, q):
-        return copy(block(y, x_lo, q), pass_send.at[y, x_lo, q], pass_recv.at[y, x_lo, q], me.at(core=1 - me.core))
+        return copy(block(y, x_lo, q), pass_send, pass_recv, other_core)
 
     def own(q):
         side_copy(q).start()
@@ -222,35 +231,25 @@
         pass_copy(1, 1, q).start()
 
     def opposite(q):
-        near_copy(0, 1, q).wait_recv()
+        copy(gathered.at[me.core, :, 0, span(q, chunks)], relay_send, rest_recv.at[q], beside_device).wait_recv()
         pass_copy(1, 0, q).start()
-        near_copy(1, 0, q).wait_recv()
         pass_copy(3, 1, q).start()
-        for way in (0, 1):
-            relay_copy(way, q).wait_recv()
-            pass_copy(2, way, q).start()
+        pass_copy(2, 0, q).start()
+        pass_copy(2, 1, q).start()
 
     def drain():
-        for q in range(chunks):
-            for y in range(4):
-                for x_lo in range(2):
-                    pass_copy(y, x_lo, q).wait_recv()
-        for q in range(chunks):
-            side_copy(q).wait_send()
-            for way in (0, 1):
-                near_copy(0, way, q).wait_send()
-                near_copy(1, way, q).wait_send()
-                relay_copy(way, q).wait_send()
-            for y in range(4):
-                for x_lo in range(2):
-                    pass_copy(y, x_lo, q).wait_send()
+        copy(gathered.at[1 - me.core], pass_send, pass_recv, other_core).wait_recv()
+        copy(gathered.at[me.core], pass_send, pass_recv, other_core).wait_send()
+        copy(gathered.at[me.core, :, 0], near_send, pass_recv, other_core).wait_send()
+        copy(gathered.at[me.core, 0], relay_send, pass_recv, other_core).wait_send()
+        copy(gathered.at[me.core, 0, 0], side_send, pass_recv, other_core).wait_send()
 
     return [own, beside, relay_own, relay_beside, opposite], drain
 
 
 def spread_scratch(chunks):
     dma = pltpu.SemaphoreType.DMA
-    return [dma((chunks,))] * 2 + [dma((2, 2, chunks))] * 2 + [dma((2, chunks))] * 2 + [dma((4, 2, chunks))] * 2
+    return [dma] * 4 + [dma((chunks,))] * 4 + [dma]
 
 
 def hot(ids, cell):
@@ -291,18 +290,23 @@
     )
 
     def tile_copy(bank):
-        return pltpu.make_async_copy(tiles_ref.at[bank], tiles_hbm.at[bank], tile_sem.at[bank])
+        return pltpu.make_async_copy(tiles_ref.at[bank], tiles_hbm.at[bank], tile_sem)
 
     def share_copy(i):
         return pltpu.make_async_remote_copy(
-            degree.at[peers[i]], shares.at[i], share_send.at[i], share_recv.at[i],
+            degree.at[peers[i]], shares.at[i], share_send, share_recv,
             device_id=(me.row, peers[i]), device_id_type=MESH,
+        )
+
+    def all_shares(send):
+        return pltpu.make_async_remote_copy(
+            shares, shares, send, share_recv, device_id=partner, device_id_type=MESH
         )
 
     def root_copy(i):
         block = roots.at[me.core, me.y, me.x_lo]
         return pltpu.make_async_remote_copy(
-            block, block, root_send.at[i], root_recv.at[i], device_id=friends[i], device_id_type=MESH
+            block, block, root_send, root_recv.at[i], device_id=friends[i], device_id_type=MESH
         )
 
     give_lists.start()
@@ -377,8 +381,8 @@
     for stage, q in RAW_LATE:
         stages[stage](q)
     total = degree[me.col]
+    all_shares(share_send).wait_recv()
     for i in range(15):
-        share_copy(i).wait_recv()
         total = total + shares[i]
     root = lax.rsqrt(1.0 + total)
     root_ref[...] = root
@@ -402,13 +406,11 @@
     for i in (8, 2, 6, 10, 14, 1, 7, 9, 15, 3, 5, 11, 13, 4, 12):
         root_copy(i - 1).wait_recv()
         scale_block(me.core if i < 8 else 1 - me.core, lax.rem(me.row + 8 - i % 8, 8))
-    for i in range(15):
-        share_copy(i).wait_send()
-        root_copy(i).wait_send()
+    all_shares(share_send).wait_send()
+    all_shares(root_send).wait_send()
     give_lists.wait_send()
     give_meta.wait_send()
-    for bank in range(groups):
-        tile_copy(bank).wait()
+    pltpu.make_async_copy(tiles_ref, tiles_hbm, tile_sem).wait()
 
 
 RAW_MOVES = (
@@ -475,7 +477,7 @@
             pltpu.VMEM((16, 8, TILE), f32),
             pltpu.VMEM((15, 8, TILE), f32),
             pltpu.VMEM((2, 4, 2, 8, TILE), f32),
-            dma((slots // GROUP,)), dma((3,)), *[dma] * 5, *[dma((15,))] * 4,
+            dma, dma((3,)), *[dma] * 8, dma((15,)),
             *spread_scratch(RAW_CHUNK),
         ],
         compiler_params=comm_params(0, START_LIMIT),

time: 132 us -> 126 us (0.955)
  Pallas kernels: 124 us -> 118 us
    pallas_call x2, Pallas kernels: 79.4 us -> 71.1 us  [sum_parts(): pl.pallas_call(functools.partial(sum_kernel, spreads), out_shape=[hop, ga...]
    pallas_call x2, Pallas kernels: 12.5 us -> 16 us  [apply_tiles(): pl.pallas_call(functools.partial(apply_kernel, len(carried)), in_specs=[S...]
where the time goes in v3:
time: 126 us; the launch traced here: 124 us
  Pallas kernels  118 us (94%)
  local copies, waits for them, and re-layouts  4.25 us (3%)
  between operations  1.33 us (1%)
    pallas_call x2, Pallas kernels, sum_parts(): pl.pallas_call(functools.partial(sum_kernel, spreads), out_shape=[hop, ga...  71.1 us
    pallas_call x1, Pallas kernels, start(): pl.pallas_call(start_kernel, out_shape=[shape((slots // GROUP, GROUP, TIL...  31.4 us
    pallas_call x2, Pallas kernels, apply_tiles(): pl.pallas_call(functools.partial(apply_kernel, len(carried)), in_specs=[S...  16 us
    unnamed x9, local copies, waits for them, and re-layouts  4.25 us

profile of v3, /device:TPU:0, one launch (start us, length us, event | category | flops | bytes accessed | tf_op | source)
XLA Modules:
  0.0 124.0 jit_solution(1335708725424448192)
XLA Ops:
  1.3 0.0 copy-start
  1.3 1.2 copy-done
  2.5 0.0 copy-start.1
  2.5 0.9 copy-done.1
  3.5 0.0 copy-start.2
  3.5 0.7 copy-done.2
  4.1 0.0 copy-start.3
  4.1 0.7 copy-done.3
  4.8 31.4 %start_build.1 = (bf16[16,64,128,128]{3,2,1,0:T(8,128)(2,1)}, s32[2,24,128]{2,1,0:T(8,128)S(1)}, f32[8,128]{1,0:T(8,128)S(1)}, bf16[2,4,2,8,128,128]{5,4,3,2,1,0:T(8,128)(2,1)S(1)}) custom-call(s32[1,1]{1,0:T(1,128)S(6)} %copy.8.count_ref, bf16[8,128,128]{2,1,0:T(8,128)(2,1)S(1)} %bitcast.16, s32[8,128]{1,0:T(8,128)S(1)} %bitcast.17, s32[8,128]{1,0:T(8,128)S(1)} %bitcast.18, ...), custom_call_target="tpu_custom_call" | custom-call | tf_op jit(solution)/shard_map/start_build/pallas_call | solution.py:463
  36.2 7.9 %apply_tiles.2 = f32[128,128,128]{2,1,0:T(8,128)S(1)} custom-call(s32[2,24,128]{2,1,0:T(8,128)S(1)} %get-tuple-element.10.metas_ref, bf16[16,64,128,128]{3,2,1,0:T(8,128)(2,1)} %get-tuple-element.11.tiles_hbm, bf16[128,128,128]{2,1,0:T(8,128)(2,1)S(1)} %bitcast.13), custom_call_target="tpu_custom_call" | custom-call | tf_op jit(solution)/shard_map/apply_tiles/pallas_call | solution.py:543
  44.2 43.4 %sum_spread.1 = (bf16[8,128,128]{2,1,0:T(8,128)(2,1)S(1)}, bf16[2,4,2,8,128,128]{5,4,3,2,1,0:T(8,128)(2,1)S(1)}) custom-call(f32[2,4,2,8,128,128]{5,4,3,2,1,0:T(8,128)S(1)} %bitcast.10, f32[8,128]{1,0:T(8,128)S(1)} %get-tuple-element.13.root_ref), custom_call_target="tpu_custom_call" | custom-call | tf_op jit(solution)/shard_map/sum_spread/pallas_call | solution.py:557
  87.6 8.0 %apply_tiles.3 = (f32[128,128,128]{2,1,0:T(8,128)S(1)}, bf16[8,128,128]{2,1,0:T(8,128)(2,1)}) custom-call(s32[2,24,128]{2,1,0:T(8,128)S(1)} %get-tuple-element.10.metas_ref, bf16[16,64,128,128]{3,2,1,0:T(8,128)(2,1)} %get-tuple-element.11.tiles_hbm, bf16[128,128,128]{2,1,0:T(8,128)(2,1)S(1)} %bitcast.12, bf16[8,128,128]{2,1,0:T(8,128)(2,1)S(1)} %get-tuple-element.15.refs_0_), custom_call_target="tpu_custom_call" | custom-call | tf_op jit(solution)/shard_map/apply_tiles/pallas_call | solution.py:543
  95.7 27.6 %sum_last.1 = bf16[8,128,128]{2,1,0:T(8,128)(2,1)S(1)} custom-call(f32[2,4,2,8,128,128]{5,4,3,2,1,0:T(8,128)S(1)} %bitcast.11, f32[8,128]{1,0:T(8,128)S(1)} %get-tuple-element.13.root_ref), custom_call_target="tpu_custom_call" | custom-call | tf_op jit(solution)/shard_map/sum_last/pallas_call | solution.py:557
  123.3 0.7 copy.9
Async XLA Ops:
  1.3 1.2 copy-start
  2.5 0.9 copy-start.1
  3.5 0.7 copy-start.2
  4.1 0.7 copy-start.3
